TPU v7x, 32 devices: a whole 2x2x4 slice. The times are simulated.
32 devices in a mesh: dap: 8 (over z, x), cplx: 4 (over y, core).
Axes of the slice: x: 2, y: 2, z: 4, core: 2. Of those that a mesh axis runs over, the one named last changes fastest.
Arguments:
- pair: bfloat16 [96, 384, 128], P('dap', 'cplx'), parts along dimension 1, may hold values from -6 to 6
- cotangent: bfloat16 [96, 384, 128], P('dap', 'cplx'), parts along dimension 1, may hold values from -6 to 6
- residue_mask: int32 [384], P('cplx'), parts along dimension 0, may hold values 0 or 1
- chain_ids: int32 [384], P('cplx'), parts along dimension 0, may hold values from 0 to 2, never falling along the last dimension, each value on 1 to 48 neighbouring positions
- chain_embed: float32 [2, 128], replicated, may hold values from -4 to 4
- out_norm_gain: float32 [128], replicated, may hold values from 0.25 to 1.75
- out_proj: bfloat16 [128, 512], replicated, may hold values from -0.5 to 0.5
- out_gate: bfloat16 [128, 128], replicated, may hold values from -0.5 to 0.5
- out_mid_gain: float32 [128], replicated, may hold values from 0.25 to 1.75
- out_final: bfloat16 [128, 128], replicated, may hold values from -0.5 to 0.5
- in_norm_gain: float32 [128], replicated, may hold values from 0.25 to 1.75
- in_proj: bfloat16 [128, 512], replicated, may hold values from -0.5 to 0.5
- in_gate: bfloat16 [128, 128], replicated, may hold values from -0.5 to 0.5
- in_mid_gain: float32 [128], replicated, may hold values from 0.25 to 1.75
- in_final: bfloat16 [128, 128], replicated, may hold values from -0.5 to 0.5
Outputs:
- pair_grad: bfloat16 [96, 384, 128], P('dap', 'cplx'), parts along dimension 1
- grad_proj: float32 [512, 512], P('cplx'), parts along dimension 0
- grad_gate: float32 [512, 128], P('cplx'), parts along dimension 0
- grad_final: float32 [512, 128], P('cplx'), parts along dimension 0
- grad_norm_gain: float32 [512], P('cplx'), parts along dimension 0
- grad_mid_gain: float32 [512], P('cplx'), parts along dimension 0
There are 4 independent parts, one for each index of `cplx`. A program takes and returns all parts, laid end to end along the dimension named above; an argument that names none is the same for every part. Nothing has to cross between parts.
Inputs may be any that keep to these rules, and one draw needn't show every extreme that they name: `chain_ids`: chain numbers never fall along the residues; each chain has at most 48 residues.
All inputs are finite; a program needn't handle non-finite values.
Results may differ from a plain program's by a relative error of at most 0.019.
Values may be sent and summed in bfloat16 or wider, within the bound.
A program may use at most 128 MiB of HBM per device.

v0:
```python
import jax
import jax.numpy as jnp
from jax import lax
from jax.sharding import PartitionSpec as P


def layer_norm(values_in, gain):
    average = jnp.mean(values_in, axis=-1, keepdims=True)
    centred = values_in - average
    variance = jnp.mean(centred * centred, axis=-1, keepdims=True)
    return centred * lax.rsqrt(variance + 1e-05) * gain


def gated_pair(projected, pair_mask, hidden_width):
    masked = pair_mask[..., None]
    left_act = (
        masked
        * jax.nn.sigmoid(projected[..., :hidden_width])
        * projected[..., hidden_width : 2 * hidden_width]
    )
    right_act = (
        masked
        * jax.nn.sigmoid(projected[..., 2 * hidden_width : 3 * hidden_width])
        * projected[..., 3 * hidden_width :]
    )
    return (left_act, right_act)


def shards(
    pair,
    cotangent,
    residue_mask,
    chain_ids,
    chain_embed,
    out_norm_gain,
    out_proj,
    out_gate,
    out_mid_gain,
    out_final,
    in_norm_gain,
    in_proj,
    in_gate,
    in_mid_gain,
    in_final,
):
    f32 = jnp.float32
    bf16 = jnp.bfloat16
    row_count = pair.shape[0]
    res_count = pair.shape[1]
    hidden_width = out_final.shape[0]
    inv_count = 1.0 / res_count
    row_start = lax.axis_index("dap") * row_count
    row_mask = lax.dynamic_slice_in_dim(residue_mask, row_start, row_count, 0)
    row_chain = lax.dynamic_slice_in_dim(chain_ids, row_start, row_count, 0)
    pair_mask = (row_mask[:, None] * residue_mask[None, :]).astype(f32)
    same_chain = row_chain[:, None] == chain_ids[None, :]
    start = pair.astype(f32) + jnp.where(same_chain[..., None], chain_embed[1], chain_embed[0])
    out_normed = layer_norm(start, out_norm_gain).astype(bf16)
    projected = jnp.dot(out_normed, out_proj, preferred_element_type=f32)
    left_act, right_act = gated_pair(projected, pair_mask, hidden_width)
    left_b = left_act.astype(bf16)
    right_b = right_act.astype(bf16)
    x_out = jnp.einsum(
        "ikc,jkc->ijc",
        left_b,
        lax.all_gather(right_b, "dap", axis=0, tiled=True),
        preferred_element_type=f32,
    )
    y_out = layer_norm(x_out, out_mid_gain).astype(bf16)
    update = jax.nn.sigmoid(jnp.dot(out_normed, out_gate, preferred_element_type=f32)) * jnp.dot(
        y_out, out_final, preferred_element_type=f32
    )
    pair_mid = (start + update).astype(bf16)
    mid_f32 = pair_mid.astype(f32)
    normed_f32, norm_back = jax.vjp(layer_norm, mid_f32, in_norm_gain)
    in_normed = normed_f32.astype(bf16)
    proj_in = jnp.dot(in_normed, in_proj, preferred_element_type=f32)
    (left_in, right_in), glu_back = jax.vjp(
        lambda proj_val: gated_pair(proj_val, pair_mask, hidden_width), proj_in
    )
    left_ib = left_in.astype(bf16)
    right_ib = right_in.astype(bf16)
    columns = lax.all_to_all(left_ib, "dap", split_axis=1, concat_axis=0, tiled=True)
    left_block = columns
    x_in = jnp.einsum(
        "kic,kjc->ijc",
        left_block,
        lax.all_gather(right_ib, "dap", axis=0, tiled=True),
        preferred_element_type=f32,
    )
    y_f32, mid_back = jax.vjp(layer_norm, x_in, in_mid_gain)
    y_in = y_f32.astype(bf16)
    logit = jnp.dot(in_normed, in_gate, preferred_element_type=f32)
    value = jnp.dot(y_in, in_final, preferred_element_type=f32)
    sigma = jax.nn.sigmoid(logit)
    upstream = cotangent.astype(f32)
    grad_value = (upstream * sigma).astype(bf16)
    grad_logit = (upstream * value * sigma * (1.0 - sigma)).astype(bf16)
    grad_final = jnp.einsum("ijc,ijd->cd", y_in, grad_value, preferred_element_type=f32) * inv_count
    grad_gate = (
        jnp.einsum("ijc,ijd->cd", in_normed, grad_logit, preferred_element_type=f32) * inv_count
    )
    grad_y = jnp.dot(grad_value, in_final.T, preferred_element_type=f32)
    grad_x, grad_mid = mid_back(grad_y)
    grad_x_b = grad_x.astype(bf16)
    shard_rows = lax.all_gather(grad_x_b, "dap", axis=0, tiled=True)
    left_block = left_ib
    grad_right = jnp.einsum("kic,ijc->kjc", left_block, shard_rows, preferred_element_type=f32)
    new_block = jnp.einsum("kjc,ijc->kic", right_ib, shard_rows, preferred_element_type=f32)
    grad_p = glu_back((new_block, grad_right))[0].astype(bf16)
    grad_proj = jnp.einsum("ijc,ijd->cd", in_normed, grad_p, preferred_element_type=f32) * inv_count
    grad_normed = jnp.dot(grad_p, in_proj.T, preferred_element_type=f32) + jnp.dot(
        grad_logit, in_gate.T, preferred_element_type=f32
    )
    grad_z, grad_norm = norm_back(grad_normed)
    pair_grad = (upstream + grad_z).astype(bf16)
    reduced = (
        lax.psum(grad_proj.astype(jnp.bfloat16), "dap").astype(jnp.float32),
        lax.psum(grad_gate.astype(jnp.bfloat16), "dap").astype(jnp.float32),
        lax.psum(grad_final.astype(jnp.bfloat16), "dap").astype(jnp.float32),
        lax.psum((grad_norm * inv_count).astype(jnp.bfloat16), "dap").astype(jnp.float32),
        lax.psum((grad_mid * inv_count).astype(jnp.bfloat16), "dap").astype(jnp.float32),
    )
    return (pair_grad, reduced[0], reduced[1], reduced[2], reduced[3], reduced[4])


def solution(mesh):
    placed = (
        P("dap", "cplx", None),
        P("dap", "cplx", None),
        P("cplx"),
        P("cplx"),
        P(),
        P(),
        P(),
        P(),
        P(),
        P(),
        P(),
        P(),
        P(),
        P(),
        P(),
    )
    return jax.shard_map(
        shards,
        mesh=mesh,
        in_specs=placed,
        out_specs=(
            P("dap", "cplx", None),
            P("cplx", None),
            P("cplx", None),
            P("cplx", None),
            P("cplx"),
            P("cplx"),
        ),
        check_vma=False,
    )
```

profile of v0, /device:TPU:0, one launch (start us, length us, event | category | flops | bytes accessed | tf_op | source)
XLA Modules:
  0.0 371.3 jit_solution(1143531026395006253)
XLA Ops:
  7.2 0.7 dynamic_slice.7
  8.0 0.7 broadcast_compare_fusion
  8.7 0.8 slice_bitcast_fusion.1
  9.5 1.4 fusion.41
  10.9 1.6 multiply_reduce_fusion.7
  12.5 0.7 dynamic_slice.6
  13.2 0.7 multiply_convert_fusion.10
  13.9 1.9 fusion.47
  15.9 1.1 fusion.28
  17.0 1.2 copy.47
  18.3 1.7 fusion.8
  19.9 51.8 %all-gather.4.cloned.1.call-done = bf16[96,96,128]{2,1,0:T(8,128)(2,1)} async-done(((bf16[12,96,128]{2,1,0:T(8,128)(2,1)}), bf16[96,96,128]{2,1,0:T(8,128)(2,1)}) %all-gather.4.cloned.1.call-update) | async-done | bytes 2359312 | tf_op jit(solution)/shard_map/all_gather | solution.py:66
  71.7 3.5 copy.46
  75.2 2.8 fusion.62
  78.5 0.5 copy-done.6
  79.2 0.6 fusion.63
  79.9 0.5 multiply_reduce_fusion.6
  80.3 0.3 copy-done.2
  80.7 0.4 multiply_convert_fusion.4
  81.1 0.4 fusion.45
  81.5 1.4 copy-done.1
  82.9 1.1 multiply_convert_fusion.2
  84.0 0.9 copy.49
  84.9 3.5 all-to-all-start
  88.4 1.1 fusion.5
  89.5 17.3 %all-to-all-done = bf16[12,96,128]{2,0,1:T(8,128)(2,1)S(1)} async-done(((bf16[12,96,128]{2,0,1:T(8,128)(2,1)}), bf16[12,96,128]{2,0,1:T(8,128)(2,1)S(1)}, u32[]{:S(2)}, u32[]{:S(2)}) %all-to-all-start) | async-done | bytes 294944 | tf_op jit(solution)/shard_map/all_to_all | solution.py:83
  107.0 1.2 copy.53
  108.2 29.5 %all-gather.6.cloned.1.call-done = bf16[96,96,128]{2,1,0:T(8,128)(2,1)} async-done(((bf16[12,96,128]{2,1,0:T(8,128)(2,1)}), bf16[96,96,128]{2,1,0:T(8,128)(2,1)}) %all-gather.6.cloned.1.call-update) | async-done | bytes 2359312 | tf_op jit(solution)/shard_map/all_gather | solution.py:88
  137.7 3.5 copy.52
  141.3 3.0 fusion.64
  144.2 1.6 copy.54
  145.8 0.3 bitcast_reduce_fusion
  146.2 0.7 multiply_reduce_fusion.5
  146.9 0.8 multiply_reduce_fusion.1
  147.7 1.5 add_convert_fusion.1
  149.4 1.2 copy.59
  150.6 1.2 copy.56
  151.8 0.5 multiply_convert_fusion.11
  152.3 0.5 fusion.9
  152.8 0.7 copy-done.12
  153.5 0.9 fusion.16
  154.4 1.3 fusion.17
  155.7 44.1 %all-gather.8.cloned.1.call-done = bf16[96,96,128]{2,1,0:T(8,128)(2,1)} async-done(((bf16[12,96,128]{2,1,0:T(8,128)(2,1)}), bf16[96,96,128]{2,1,0:T(8,128)(2,1)}) %all-gather.8.cloned.1.call-update) | async-done | bytes 2359312 | tf_op jit(solution)/shard_map/all_gather | solution.py:106
  199.8 3.5 copy.55
  203.3 3.8 %fusion.66 = f32[128,96,12]{1,2,0:T(8,128)} fusion(bf16[96,96,128]{1,0,2:T(8,128)(2,1)S(1)} %copy.55, bf16[12,96,128]{1,0,2:T(8,128)(2,1)} %copy.59), kind=kOutput, calls=%fused_computation.126 | convolution fusion | flops 28311552 | bytes 3244032 | tf_op jit(solution)/shard_map/kjc,ijc->kic/dot_general | solution.py:109
  207.1 2.4 copy.60
  209.4 2.9 fusion.65
  212.4 1.5 copy.57
  213.9 2.4 bitcast_multiply_fusion.3
  216.3 0.5 fusion.43
  216.8 0.5 copy-done.16
  217.3 1.0 fusion.13
  218.4 0.5 multiply_reduce_fusion.3
  218.9 0.8 multiply_reduce_fusion.2
  219.7 0.5 multiply_convert_fusion.12
  220.3 0.5 all-reduce.8.cloned.1.call-update
  220.8 1.5 fusion.19
  222.3 66.6 %all-reduce.10.cloned.1.call-done = (bf16[128,128]{1,0:T(8,128)(2,1)}, bf16[128,128]{1,0:T(8,128)(2,1)}, bf16[128]{0:T(256)(128)(2,1)}, bf16[128]{0:T(256)(128)(2,1)}) async-done(((bf16[128,128]{1,0:T(8,128)(2,1)}, bf16[128,128]{1,0:T(8,128)(2,1)}, bf16[128]{0:T(256)(128)(2,1)}, bf16[128]{0:T(256)(128)(2,1)}), (bf16[128,128]{1,0:T(8,128)(2,1)}, bf16[128,128]{1,0:T(8,128)(2,1)}, bf16[128]{0:T(256)(128)(2,1)}, ...) | async-done | bytes 66064 | tf_op jit(solution)/shard_map/psum | solution.py:119
  288.9 1.4 convert_element_type.109
  290.3 1.4 convert_element_type.111
  291.7 1.1 convert_element_type.113
  292.8 1.1 convert_element_type.115
  293.9 69.3 %all-reduce.8.cloned.1.call-done = bf16[128,512]{1,0:T(8,128)(2,1)} async-done(((bf16[128,512]{1,0:T(8,128)(2,1)}), bf16[128,512]{1,0:T(8,128)(2,1)}) %all-reduce.8.cloned.1.call-update) | async-done | bytes 131088 | tf_op jit(solution)/shard_map/psum | solution.py:118
  363.2 1.6 convert_element_type.107
  (71 shorter events, 1.4 us)
Async XLA Ops:
  7.2 73.9 %copy-start = (bf16[128,512]{1,0:T(8,128)(2,1)S(1)}, bf16[128,512]{1,0:T(8,128)(2,1)}, u32[]{:S(2)}) copy-start(bf16[128,512]{1,0:T(8,128)(2,1)} %param.26) | copy-start | bytes 393220
  7.2 64.5 %all-gather.4.cloned.1.call-start = ((), (), s32[]{:S(2)}) async-start(), calls=%async_computation.1 | async-start | bytes 2654208 | tf_op jit(solution)/shard_map/all_gather | solution.py:66
  15.9 2.4 copy-start.5
  15.9 2.4 copy-start.23
  15.9 2.4 copy-start.25
  17.0 120.7 %all-gather.6.cloned.1.call-start = ((), (), s32[]{:S(2)}) async-start(), calls=%async_computation.2 | async-start | bytes 2654208 | tf_op jit(solution)/shard_map/all_gather | solution.py:88
  75.2 3.1 copy-start.24
  78.0 1.0 copy-start.6
  78.0 1.2 copy-start.17
  78.0 1.2 copy-start.19
  78.1 2.6 copy-start.22
  79.8 0.8 copy-start.2
  81.1 7.4 %copy-start.14 = (bf16[12,96,128]{2,1,0:T(8,128)(2,1)}, bf16[12,96,128]{2,1,0:T(8,128)(2,1)S(1)}, u32[]{:S(2)}) copy-start(bf16[12,96,128]{2,1,0:T(8,128)(2,1)S(1)} %multiply_convert_fusion.4) | copy-start | bytes 884740
  81.5 1.4 copy-start.1
  82.9 5.5 %copy-start.20 = (bf16[128,128]{1,0:T(8,128)(2,1)S(1)}, bf16[128,128]{1,0:T(8,128)(2,1)}, u32[]{:S(2)}) copy-start(bf16[128,128]{1,0:T(8,128)(2,1)} %param.27) | copy-start | bytes 98308
  84.0 22.9 %copy-start.9 = (bf16[12,96,128]{2,1,0:T(8,128)(2,1)}, bf16[12,96,128]{2,1,0:T(8,128)(2,1)S(1)}, u32[]{:S(2)}) copy-start(bf16[12,96,128]{2,1,0:T(8,128)(2,1)S(1)} %get-tuple-element.22) | copy-start | bytes 884740
  84.9 22.0 %all-to-all-start = ((bf16[12,96,128]{2,0,1:T(8,128)(2,1)}), bf16[12,96,128]{2,0,1:T(8,128)(2,1)S(1)}, u32[]{:S(2)}, u32[]{:S(2)}) async-start(bf16[12,96,128]{2,0,1:T(8,128)(2,1)} %copy.49), calls=%async_computation | async-start | bytes 786432 | tf_op jit(solution)/shard_map/all_to_all | solution.py:83
  88.4 111.4 %all-gather.8.cloned.1.call-start = ((), (), s32[]{:S(2)}) async-start(), calls=%async_computation.3 | async-start | bytes 2654208 | tf_op jit(solution)/shard_map/all_gather | solution.py:106
  141.2 4.9 %copy-start.18 = (bf16[128,128]{1,0:T(8,128)(2,1)S(1)}, bf16[128,128]{1,0:T(8,128)(2,1)}, u32[]{:S(2)}) copy-start(bf16[128,128]{1,0:T(8,128)(2,1)} %param.29) | copy-start | bytes 98308
  141.2 4.9 %copy-start.21 = (f32[128]{0:T(128)S(1)}, f32[128]{0:T(128)}, u32[]{:S(2)}) copy-start(f32[128]{0:T(128)} %param.28) | copy-start | bytes 1540
  144.2 1.9 copy-start.4
  144.2 1.9 copy-start.7
  146.2 3.2 copy-start.11
  146.9 3.7 %copy-start.10 = (bf16[12,96,128]{2,1,0:T(8,128)(2,1)S(1)}, bf16[12,96,128]{2,1,0:T(8,128)(2,1)}, u32[]{:S(2)}) copy-start(bf16[12,96,128]{2,1,0:T(8,128)(2,1)} %copy-done.9) | copy-start | bytes 884740
  147.7 5.9 %copy-start.15 = (bf16[12,96,128]{2,1,0:T(8,128)(2,1)S(1)}, bf16[12,96,128]{2,1,0:T(8,128)(2,1)}, u32[]{:S(2)}) copy-start(bf16[12,96,128]{2,1,0:T(8,128)(2,1)} %copy-done.14) | copy-start | bytes 884740
  149.2 139.7 %all-reduce.10.cloned.1.call-start = ((), (), s32[]{:S(2)}) async-start(), calls=%async_computation.5 | async-start | bytes 133120 | tf_op jit(solution)/shard_map/psum | solution.py:119
  152.8 0.7 copy-start.12
  216.3 1.0 copy-start.16
  217.3 1.1 copy-start.3
  217.3 1.1 copy-start.13
  218.3 2.5 copy-start.8
  220.2 143.0 %all-reduce.8.cloned.1.call-start = ((), (), s32[]{:S(2)}) async-start(), calls=%async_computation.4 | async-start | bytes 262144 | tf_op jit(solution)/shard_map/psum | solution.py:118
Sparse Core Ops, SparseCore 0:
  17.1 54.5 all-gather.3
  84.1 53.5 all-gather.5
  149.3 50.4 all-gather.7
  220.3 68.4 all-reduce.9
  292.6 70.4 all-reduce.7
where the time goes:
time: 372 us; the launch traced here: 371 us
  waiting for transfers between devices  279 us (75%)
  local copies, waits for them, and re-layouts  27.9 us (8%)
  matrix products  23.6 us (6%)
  other arithmetic  22.7 us (6%)
  between operations  14.2 us (4%)
  starting transfers between devices  3.84 us (1%)
    psum x1, waiting for transfers between devices, shards(): lax.psum(grad_proj.astype(jnp.bfloat16), 'dap').astype(jnp.float32)  69.3 us
    psum x1, waiting for transfers between devices, shards(): lax.psum(grad_gate.astype(jnp.bfloat16), 'dap').astype(jnp.float32)  66.6 us
    all_gather x1, waiting for transfers between devices, shards(): lax.all_gather(right_b, 'dap', axis=0, tiled=True)  51.8 us
    all_gather x1, waiting for transfers between devices, shards(): shard_rows = lax.all_gather(grad_x_b, 'dap', axis=0, tiled=True)  44.1 us
    all_gather x1, waiting for transfers between devices, shards(): lax.all_gather(right_ib, 'dap', axis=0, tiled=True)  29.5 us
    all_to_all x1, waiting for transfers between devices, shards(): lax.all_to_all(left_ib, 'dap', split_axis=1, concat_axis=0, tiled=True)  17.3 us
  transfers between devices with their start and end apart: 6, of which 6 were waited for; matrix products, arithmetic and copies ran while one was open for 5% of the time, Pallas kernels for 0%

commit v1 on v0

--- a/solution.py
+++ b/solution.py
@@ -82,12 +82,27 @@
     right_ib = right_in.astype(bf16)
     columns = lax.all_to_all(left_ib, "dap", split_axis=1, concat_axis=0, tiled=True)
     left_block = columns
-    x_in = jnp.einsum(
-        "kic,kjc->ijc",
-        left_block,
-        lax.all_gather(right_ib, "dap", axis=0, tiled=True),
-        preferred_element_type=f32,
+    piece_next, block_last, far_arr = (
+        lax.axis_size("dap"),
+        lax.axis_index("dap"),
+        right_ib.shape[0],
     )
+    pool = [(t, (t + 1) % piece_next) for t in range(piece_next)]
+    back, x_in = (right_ib, None)
+    at = 0
+    while at < piece_next:
+        outcome_arr = lax.ppermute(back, "dap", perm=pool) if at < piece_next - 1 else None
+        then = jnp.einsum(
+            "kic,kjc->ijc",
+            lax.dynamic_slice_in_dim(
+                left_block, (block_last - at) % piece_next * far_arr, back.shape[0], axis=0
+            ),
+            back,
+            preferred_element_type=f32,
+        )
+        x_in = then if x_in is None else x_in + then
+        back = outcome_arr
+        at += 1
     y_f32, mid_back = jax.vjp(layer_norm, x_in, in_mid_gain)
     y_in = y_f32.astype(bf16)
     logit = jnp.dot(in_normed, in_gate, preferred_element_type=f32)

time: 372 us -> 399 us (1.073)
  local copies, waits for them, and re-layouts: 27.9 us -> 50.4 us
  waiting for transfers between devices: 279 us -> 266 us
  starting transfers between devices: 3.84 us -> 15.3 us
  matrix products: 23.6 us -> 27.8 us
    all_gather x1 -> x0, waiting for transfers between devices: 29.5 us -> none  [shards(): lax.all_gather(right_ib, 'dap', axis=0, tiled=True)]
    ppermute x0 -> x7, waiting for transfers between devices: none -> 23.1 us  [shards(): lax.ppermute(back, 'dap', perm=pool)]
    ppermute x0 -> x7, local copies, waits for them, and re-layouts: none -> 11.8 us  [shards(): lax.ppermute(back, 'dap', perm=pool)]
    ppermute x0 -> x7, starting transfers between devices: none -> 8.91 us  [shards(): lax.ppermute(back, 'dap', perm=pool)]
    unnamed x52 -> x88, local copies, waits for them, and re-layouts: 3.78 us -> 12.2 us
    dot_general x1 -> x8, local copies, waits for them, and re-layouts: 1.62 us -> 8.65 us  [shards(): jnp.einsum('kic,kjc->ijc', lax.dynamic_slice_in_dim(left_block, (block_la...]
    all_to_all x1, waiting for transfers between devices: 17.3 us -> 11.3 us  [shards(): lax.all_to_all(left_ib, 'dap', split_axis=1, concat_axis=0, tiled=True)]
    dot_general x1 -> x8, matrix products: 2.96 us -> 7.94 us  [shards(): jnp.einsum('kic,kjc->ijc', lax.dynamic_slice_in_dim(left_block, (block_la...]
  transfers between devices with their start and end apart: 6 -> 12, of which waited for: 6 -> 10; matrix products, arithmetic and copies ran while one was open for 5% -> 12% of each run, Pallas kernels for 0% -> 0%
where the time goes in v1:
time: 399 us; the launch traced here: 398 us
  waiting for transfers between devices  266 us (67%)
  local copies, waits for them, and re-layouts  50.4 us (13%)
  matrix products  27.8 us (7%)
  other arithmetic  23.8 us (6%)
  starting transfers between devices  15.3 us (4%)
  between operations  14.4 us (4%)
    psum x1, waiting for transfers between devices, shards(): lax.psum(grad_proj.astype(jnp.bfloat16), 'dap').astype(jnp.float32)  69.2 us
    psum x1, waiting for transfers between devices, shards(): lax.psum(grad_gate.astype(jnp.bfloat16), 'dap').astype(jnp.float32)  66.6 us
    all_gather x1, waiting for transfers between devices, shards(): lax.all_gather(right_b, 'dap', axis=0, tiled=True)  51.9 us
    all_gather x1, waiting for transfers between devices, shards(): shard_rows = lax.all_gather(grad_x_b, 'dap', axis=0, tiled=True)  43.8 us
    ppermute x7, waiting for transfers between devices, shards(): lax.ppermute(back, 'dap', perm=pool)  23.1 us
    unnamed x88, local copies, waits for them, and re-layouts  12.2 us
    ppermute x7, local copies, waits for them, and re-layouts, shards(): lax.ppermute(back, 'dap', perm=pool)  11.8 us
    all_to_all x1, waiting for transfers between devices, shards(): lax.all_to_all(left_ib, 'dap', split_axis=1, concat_axis=0, tiled=True)  11.3 us
  transfers between devices with their start and end apart: 12, of which 10 were waited for; matrix products, arithmetic and copies ran while one was open for 12% of the time, Pallas kernels for 0%

profile of v1, /device:TPU:0, one launch (start us, length us, event | category | flops | bytes accessed | tf_op | source)
XLA Modules:
  0.0 398.1 jit_solution(5873088333459473506)
XLA Ops:
  9.4 1.4 fusion.41
  10.9 1.6 multiply_reduce_fusion.7
  13.9 1.9 fusion.47
  15.9 1.1 fusion.28
  17.0 1.2 copy.82
  18.2 1.6 fusion.8
  19.8 51.9 %all-gather.3.cloned.1.call-done = bf16[96,96,128]{2,1,0:T(8,128)(2,1)} async-done(((bf16[12,96,128]{2,1,0:T(8,128)(2,1)}), bf16[96,96,128]{2,1,0:T(8,128)(2,1)}) %all-gather.3.cloned.1.call-update) | async-done | bytes 2359312 | tf_op jit(solution)/shard_map/all_gather | solution.py:66
  71.7 3.5 copy.81
  75.2 2.8 fusion.62
  81.5 1.4 copy-done.1
  83.9 9.4 %collective-permute-done = bf16[12,96,128]{2,1,0:T(8,128)(2,1)S(1)} collective-permute-done((bf16[12,96,128]{2,1,0:T(8,128)(2,1)S(1)}, bf16[12,96,128]{2,1,0:T(8,128)(2,1)S(1)}, u32[]{:S(2)}, u32[]{:S(2)}) %collective-permute-start) | collective-permute-done | bytes 294944 | tf_op jit(solution)/shard_map/ppermute | solution.py:94
  93.3 0.9 copy.84
  94.2 6.0 %all-to-all-start = ((bf16[12,96,128]{2,0,1:T(8,128)(2,1)}), bf16[12,96,128]{2,0,1:T(8,128)(2,1)S(1)}, u32[]{:S(2)}, u32[]{:S(2)}) async-start(bf16[12,96,128]{2,0,1:T(8,128)(2,1)} %copy.84), calls=%async_computation | async-start | bytes 786432 | tf_op jit(solution)/shard_map/all_to_all | solution.py:83
  100.2 2.8 collective-permute-done.1
  104.2 11.3 %all-to-all-done = bf16[12,96,128]{2,0,1:T(8,128)(2,1)S(1)} async-done(((bf16[12,96,128]{2,0,1:T(8,128)(2,1)}), bf16[12,96,128]{2,0,1:T(8,128)(2,1)S(1)}, u32[]{:S(2)}, u32[]{:S(2)}) %all-to-all-start) | async-done | bytes 294944 | tf_op jit(solution)/shard_map/all_to_all | solution.py:83
  115.6 5.8 %collective-permute-start.3 = (bf16[12,96,128]{2,1,0:T(8,128)(2,1)}, bf16[12,96,128]{2,1,0:T(8,128)(2,1)}, u32[]{:S(2)}, u32[]{:S(2)}) collective-permute-start(bf16[12,96,128]{2,1,0:T(8,128)(2,1)} %collective-permute-done.2), channel_id=1, source_target_pairs={{0,4},{4,8},{8,12},{12,16},{16,20},{20,24},{24,28},{28,0},{1,5},{5... | collective-permute-start | bytes 884744 | tf_op jit(solution)/shard_map/ppermute | solution.py:94
  122.7 1.2 copy.119
  124.2 4.5 %collective-permute-done.3 = bf16[12,96,128]{2,1,0:T(8,128)(2,1)} collective-permute-done((bf16[12,96,128]{2,1,0:T(8,128)(2,1)}, bf16[12,96,128]{2,1,0:T(8,128)(2,1)}, u32[]{:S(2)}, u32[]{:S(2)}) %collective-permute-start.3) | collective-permute-done | bytes 294944 | tf_op jit(solution)/shard_map/ppermute | solution.py:94
  128.7 2.5 collective-permute-start.4
  131.5 2.0 copy.121
  133.5 1.2 copy.92
  134.6 1.2 copy.91
  135.8 1.3 copy.122
  137.1 1.3 copy.123
  139.3 1.2 copy.126
  140.5 1.2 copy.94
  141.8 1.3 fusion.66
  143.4 2.2 copy.97
  145.6 1.5 fusion.67
  147.1 1.2 copy.98
  148.3 2.2 copy.100
  150.5 1.5 fusion.68
  152.0 1.2 copy.101
  153.1 2.2 copy.103
  155.3 2.1 collective-permute-done.5
  157.5 1.3 fusion.69
  158.8 1.2 copy.104
  160.0 1.4 copy.106
  161.7 1.2 copy.107
  162.9 4.3 %collective-permute-done.6 = bf16[12,96,128]{2,1,0:T(8,128)(2,1)} collective-permute-done((bf16[12,96,128]{2,1,0:T(8,128)(2,1)}, bf16[12,96,128]{2,1,0:T(8,128)(2,1)}, u32[]{:S(2)}, u32[]{:S(2)}) %collective-permute-start.6) | collective-permute-done | bytes 294944 | tf_op jit(solution)/shard_map/ppermute | solution.py:94
  167.2 2.2 copy.109
  169.4 1.5 fusion.71
  170.9 1.2 copy.110
  172.1 2.1 bitcast_reduce_fusion
  175.8 1.4 add_convert_fusion.1
  177.5 1.2 copy.112
  180.4 0.9 fusion.16
  181.3 1.3 fusion.17
  182.6 43.8 %all-gather.5.cloned.1.call-done = bf16[96,96,128]{2,1,0:T(8,128)(2,1)} async-done(((bf16[12,96,128]{2,1,0:T(8,128)(2,1)}), bf16[96,96,128]{2,1,0:T(8,128)(2,1)}) %all-gather.5.cloned.1.call-update) | async-done | bytes 2359312 | tf_op jit(solution)/shard_map/all_gather | solution.py:121
  226.4 3.5 copy.111
  230.0 3.8 fusion.73
  233.7 2.4 copy.116
  236.1 3.0 fusion.72
  239.1 1.5 copy.113
  240.6 2.4 bitcast_multiply_fusion.3
  244.0 1.0 fusion.13
  247.5 1.5 fusion.19
  249.0 66.6 %all-reduce.10.cloned.1.call-done = (bf16[128,128]{1,0:T(8,128)(2,1)}, bf16[128,128]{1,0:T(8,128)(2,1)}, bf16[128]{0:T(256)(128)(2,1)}, bf16[128]{0:T(256)(128)(2,1)}) async-done(((bf16[128,128]{1,0:T(8,128)(2,1)}, bf16[128,128]{1,0:T(8,128)(2,1)}, bf16[128]{0:T(256)(128)(2,1)}, bf16[128]{0:T(256)(128)(2,1)}), (bf16[128,128]{1,0:T(8,128)(2,1)}, bf16[128,128]{1,0:T(8,128)(2,1)}, bf16[128]{0:T(256)(128)(2,1)}, ...) | async-done | bytes 66064 | tf_op jit(solution)/shard_map/psum | solution.py:134
  315.6 1.4 convert_element_type.109
  317.0 1.4 convert_element_type.111
  318.4 1.2 convert_element_type.113
  319.5 1.1 convert_element_type.115
  320.7 69.2 %all-reduce.8.cloned.1.call-done = bf16[128,512]{1,0:T(8,128)(2,1)} async-done(((bf16[128,512]{1,0:T(8,128)(2,1)}), bf16[128,512]{1,0:T(8,128)(2,1)}) %all-reduce.8.cloned.1.call-update) | async-done | bytes 131088 | tf_op jit(solution)/shard_map/psum | solution.py:133
  389.9 1.6 convert_element_type.107
  (138 shorter events, 19.7 us)
Async XLA Ops:
  7.2 73.9 %copy-start = (bf16[128,512]{1,0:T(8,128)(2,1)S(1)}, bf16[128,512]{1,0:T(8,128)(2,1)}, u32[]{:S(2)}) copy-start(bf16[128,512]{1,0:T(8,128)(2,1)} %param.26) | copy-start | bytes 393220
  7.2 64.5 %all-gather.3.cloned.1.call-start = ((), (), s32[]{:S(2)}) async-start(), calls=%async_computation.1 | async-start | bytes 2654208 | tf_op jit(solution)/shard_map/all_gather | solution.py:66
  13.9 67.6 %copy-start.26 = (f32[12,96]{1,0:T(8,128)}, f32[12,96]{1,0:T(8,128)S(1)}, u32[]{:S(2)}) copy-start(f32[12,96]{1,0:T(8,128)S(1)} %multiply_convert_fusion.10) | copy-start | bytes 13828
  15.9 2.3 copy-start.4
  15.9 2.3 copy-start.37
  15.9 2.3 copy-start.39
  75.2 3.1 copy-start.38
  78.0 1.0 copy-start.5
  78.0 1.2 copy-start.20
  78.0 1.2 copy-start.30
  78.1 2.6 copy-start.35
  79.8 0.8 copy-start.2
  80.3 3.0 copy-start.28
  81.1 22.4 %copy-start.13 = (bf16[12,96,128]{2,1,0:T(8,128)(2,1)}, bf16[12,96,128]{2,1,0:T(8,128)(2,1)S(1)}, u32[]{:S(2)}) copy-start(bf16[12,96,128]{2,1,0:T(8,128)(2,1)S(1)} %multiply_convert_fusion.4) | copy-start | bytes 884740
  81.5 1.4 copy-start.1
  82.9 20.5 %copy-start.31 = (bf16[128,128]{1,0:T(8,128)(2,1)S(1)}, bf16[128,128]{1,0:T(8,128)(2,1)}, u32[]{:S(2)}) copy-start(bf16[128,128]{1,0:T(8,128)(2,1)} %param.27) | copy-start | bytes 98308
  83.3 10.0 %copy-start.9 = (bf16[12,96,128]{2,1,0:T(8,128)(2,1)}, bf16[12,96,128]{2,1,0:T(8,128)(2,1)S(1)}, u32[]{:S(2)}) copy-start(bf16[12,96,128]{2,1,0:T(8,128)(2,1)S(1)} %get-tuple-element.24) | copy-start | bytes 884740
  83.3 10.0 %collective-permute-start = (bf16[12,96,128]{2,1,0:T(8,128)(2,1)S(1)}, bf16[12,96,128]{2,1,0:T(8,128)(2,1)S(1)}, u32[]{:S(2)}, u32[]{:S(2)}) collective-permute-start(bf16[12,96,128]{2,1,0:T(8,128)(2,1)S(1)} %get-tuple-element.25), channel_id=1, source_target_pairs={{0,4},{4,8},{8,12},{12,16},{16,20},{20,24},{24,28},{28,0},{1,5},{5... | collective-permute-start | bytes 884744 | tf_op jit(solution)/shard_map/ppermute | solution.py:94
  93.3 9.7 %collective-permute-start.1 = (bf16[12,96,128]{2,1,0:T(8,128)(2,1)S(1)}, bf16[12,96,128]{2,1,0:T(8,128)(2,1)S(1)}, u32[]{:S(2)}, u32[]{:S(2)}) collective-permute-start(bf16[12,96,128]{2,1,0:T(8,128)(2,1)S(1)} %collective-permute-done), channel_id=1, source_target_pairs={{0,4},{4,8},{8,12},{12,16},{16,20},{20,24},{24,28},{28,0},{1,5},{5... | collective-permute-start | bytes 884744 | tf_op jit(solution)/shard_map/ppermute | solution.py:94
  94.2 21.3 %all-to-all-start = ((bf16[12,96,128]{2,0,1:T(8,128)(2,1)}), bf16[12,96,128]{2,0,1:T(8,128)(2,1)S(1)}, u32[]{:S(2)}, u32[]{:S(2)}) async-start(bf16[12,96,128]{2,0,1:T(8,128)(2,1)} %copy.84), calls=%async_computation | async-start | bytes 786432 | tf_op jit(solution)/shard_map/all_to_all | solution.py:83
  100.2 126.3 %all-gather.5.cloned.1.call-start = ((), (), s32[]{:S(2)}) async-start(), calls=%async_computation.2 | async-start | bytes 2654208 | tf_op jit(solution)/shard_map/all_gather | solution.py:121
  103.0 12.5 %copy-start.21 = (bf16[12,96,128]{2,1,0:T(8,128)(2,1)}, bf16[12,96,128]{2,1,0:T(8,128)(2,1)S(1)}, u32[]{:S(2)}) copy-start(bf16[12,96,128]{2,1,0:T(8,128)(2,1)S(1)} %collective-permute-done.1) | copy-start | bytes 884740
  103.0 12.6 %collective-permute-start.2 = (bf16[12,96,128]{2,1,0:T(8,128)(2,1)S(1)}, bf16[12,96,128]{2,1,0:T(8,128)(2,1)}, u32[]{:S(2)}, u32[]{:S(2)}) collective-permute-start(bf16[12,96,128]{2,1,0:T(8,128)(2,1)S(1)} %collective-permute-done.1), channel_id=1, source_target_pairs={{0,4},{4,8},{8,12},{12,16},{16,20},{20,24},{24,28},{28,0},{1,5},{5... | collective-permute-start | bytes 884744 | tf_op jit(solution)/shard_map/ppermute | solution.py:94
  103.4 27.7 %copy-start.8 = (bf16[12,96,128]{1,0,2:T(8,128)(2,1)}, bf16[12,96,128]{1,0,2:T(8,128)(2,1)S(1)}, u32[]{:S(2)}) copy-start(bf16[12,96,128]{1,0,2:T(8,128)(2,1)S(1)} %copy.88) | copy-start | bytes 884740
  115.6 13.1 %collective-permute-start.3 = (bf16[12,96,128]{2,1,0:T(8,128)(2,1)}, bf16[12,96,128]{2,1,0:T(8,128)(2,1)}, u32[]{:S(2)}, u32[]{:S(2)}) collective-permute-start(bf16[12,96,128]{2,1,0:T(8,128)(2,1)} %collective-permute-done.2), channel_id=1, source_target_pairs={{0,4},{4,8},{8,12},{12,16},{16,20},{20,24},{24,28},{28,0},{1,5},{5... | collective-permute-start | bytes 884744 | tf_op jit(solution)/shard_map/ppermute | solution.py:94
  123.9 7.3 %copy-start.19 = (bf16[12,12,128]{0,1,2:T(8,128)(2,1)S(1)}, bf16[12,12,128]{0,1,2:T(8,128)(2,1)}, u32[]{:S(2)}) copy-start(bf16[12,12,128]{0,1,2:T(8,128)(2,1)} %copy.119) | copy-start | bytes 110596
  128.7 17.0 %collective-permute-start.4 = (bf16[12,96,128]{2,1,0:T(8,128)(2,1)}, bf16[12,96,128]{2,1,0:T(8,128)(2,1)}, u32[]{:S(2)}, u32[]{:S(2)}) collective-permute-start(bf16[12,96,128]{2,1,0:T(8,128)(2,1)} %collective-permute-done.3), channel_id=1, source_target_pairs={{0,4},{4,8},{8,12},{12,16},{16,20},{20,24},{24,28},{28,0},{1,5},{5... | collective-permute-start | bytes 884744 | tf_op jit(solution)/shard_map/ppermute | solution.py:94
  131.4 4.4 %copy-start.23 = (bf16[12,12,128]{2,0,1:T(8,128)(2,1)S(1)}, bf16[12,12,128]{2,0,1:T(8,128)(2,1)}, u32[]{:S(2)}) copy-start(bf16[12,12,128]{2,0,1:T(8,128)(2,1)} %get-tuple-element.32) | copy-start | bytes 110596
  134.6 5.9 %copy-start.22 = (bf16[12,96,128]{2,1,0:T(8,128)(2,1)S(1)}, bf16[12,96,128]{2,1,0:T(8,128)(2,1)}, u32[]{:S(2)}) copy-start(bf16[12,96,128]{2,1,0:T(8,128)(2,1)} %copy-done.21) | copy-start | bytes 884740
  135.8 5.9 %copy-start.18 = (bf16[12,12,128]{0,1,2:T(8,128)(2,1)S(1)}, bf16[12,12,128]{0,1,2:T(8,128)(2,1)}, u32[]{:S(2)}) copy-start(bf16[12,12,128]{0,1,2:T(8,128)(2,1)} %copy.121) | copy-start | bytes 110596
  145.6 11.9 %collective-permute-start.5 = (bf16[12,96,128]{2,1,0:T(8,128)(2,1)}, bf16[12,96,128]{2,1,0:T(8,128)(2,1)}, u32[]{:S(2)}, u32[]{:S(2)}) collective-permute-start(bf16[12,96,128]{2,1,0:T(8,128)(2,1)} %collective-permute-done.4), channel_id=1, source_target_pairs={{0,4},{4,8},{8,12},{12,16},{16,20},{20,24},{24,28},{28,0},{1,5},{5... | collective-permute-start | bytes 884744 | tf_op jit(solution)/shard_map/ppermute | solution.py:94
  157.5 9.7 %collective-permute-start.6 = (bf16[12,96,128]{2,1,0:T(8,128)(2,1)}, bf16[12,96,128]{2,1,0:T(8,128)(2,1)}, u32[]{:S(2)}, u32[]{:S(2)}) collective-permute-start(bf16[12,96,128]{2,1,0:T(8,128)(2,1)} %collective-permute-done.5), channel_id=1, source_target_pairs={{0,4},{4,8},{8,12},{12,16},{16,20},{20,24},{24,28},{28,0},{1,5},{5... | collective-permute-start | bytes 884744 | tf_op jit(solution)/shard_map/ppermute | solution.py:94
  162.9 9.1 %copy-start.16 = (f32[128,96,12]{0,1,2:T(8,128)S(1)}, f32[128,96,12]{0,1,2:T(8,128)}, u32[]{:S(2)}) copy-start(f32[128,96,12]{0,1,2:T(8,128)} %copy.92) | copy-start | bytes 1769476
  162.9 9.1 %copy-start.17 = (f32[128,96,12]{0,1,2:T(8,128)S(1)}, f32[128,96,12]{0,1,2:T(8,128)}, u32[]{:S(2)}) copy-start(f32[128,96,12]{0,1,2:T(8,128)} %copy.91) | copy-start | bytes 1769476
  172.1 2.2 copy-start.6
  172.1 2.2 copy-start.24
  172.1 2.2 copy-start.33
  174.2 3.3 copy-start.10
  174.9 4.3 %copy-start.25 = (bf16[128,128]{1,0:T(8,128)(2,1)S(1)}, bf16[128,128]{1,0:T(8,128)(2,1)}, u32[]{:S(2)}) copy-start(bf16[128,128]{1,0:T(8,128)(2,1)} %param.29) | copy-start | bytes 98308
  175.0 4.3 %copy-start.34 = (f32[128]{0:T(128)S(1)}, f32[128]{0:T(128)}, u32[]{:S(2)}) copy-start(f32[128]{0:T(128)} %param.28) | copy-start | bytes 1540
  175.7 4.7 %copy-start.14 = (bf16[12,96,128]{2,1,0:T(8,128)(2,1)S(1)}, bf16[12,96,128]{2,1,0:T(8,128)(2,1)}, u32[]{:S(2)}) copy-start(bf16[12,96,128]{2,1,0:T(8,128)(2,1)} %copy-done.13) | copy-start | bytes 884740
  177.2 138.4 %all-reduce.10.cloned.1.call-start = ((), (), s32[]{:S(2)}) async-start(), calls=%async_computation.4 | async-start | bytes 133120 | tf_op jit(solution)/shard_map/psum | solution.py:134
  179.7 0.7 copy-start.11
  236.1 4.5 %copy-start.27 = (f32[12,96]{1,0:T(8,128)S(1)}, f32[12,96]{1,0:T(8,128)}, u32[]{:S(2)}) copy-start(f32[12,96]{1,0:T(8,128)} %copy-done.26) | copy-start | bytes 13828
  243.0 1.0 copy-start.15
  244.0 1.1 copy-start.3
  244.0 1.1 copy-start.12
  244.0 1.1 copy-start.32
  244.0 1.1 copy-start.36
  244.0 1.6 copy-start.29
  245.0 2.5 copy-start.7
  246.9 143.0 %all-reduce.8.cloned.1.call-start = ((), (), s32[]{:S(2)}) async-start(), calls=%async_computation.3 | async-start | bytes 262144 | tf_op jit(solution)/shard_map/psum | solution.py:133
Sparse Core Ops, SparseCore 0:
  17.1 54.5 all-gather.2
  177.4 49.0 all-gather.4
  247.1 68.4 all-reduce.9
  319.4 70.4 all-reduce.7
